TPU v7x, 32 devices: a whole 2x2x4 slice. The times are simulated.
32 devices in a mesh: dp: 4 (over z), tp: 8 (over y, x, core).
Axes of the slice: x: 2, y: 2, z: 4, core: 2. Of those that a mesh axis runs over, the one named last changes fastest.
Arguments:
- layer_input: bfloat16 [8192, 2048], P(('dp', 'tp')), may hold values from -6 to 6
- segments: int32 [4, 2048], P('dp'), may hold values from 0 to 1, as said below
- norm_gains: float32 [2, 2048], replicated, may hold values from 0.25 to 1.75
- norm_biases: float32 [2, 2048], replicated, may hold values from -2 to 2
- w_qkv: bfloat16 [2048, 3, 2048], P(None, None, 'tp'), may hold values from -0.125 to 0.125
- qv_bias: float32 [2, 2048], P(None, 'tp'), may hold values from -2 to 2
- key_bias: float32 [32, 16], P('tp'), may hold values from -3 to 3
- w_out: bfloat16 [2048, 2048], P('tp'), may hold values from -2 to 2
- w_gate_up: bfloat16 [2048, 2, 5632], P(None, None, 'tp'), may hold values from -0.125 to 0.125
- w_down: bfloat16 [5632, 2048], P('tp'), may hold values from -0.078125 to 0.078125
- out_grad: bfloat16 [8192, 2048], P(('dp', 'tp')), may hold values from -6 to 6
Outputs:
- output: float32 [8192, 2048], P(('dp', 'tp'))
- grad_x: float32 [8192, 2048], P(('dp', 'tp'))
- grad_qkv: float32 [2048, 3, 2048], P(None, None, 'tp')
- grad_qv_bias: float32 [2, 2048], P(None, 'tp')
- grad_key_bias: float32 [32, 16], P('tp')
- grad_out: float32 [2048, 2048], P('tp')
- grad_gate_up: float32 [2048, 2, 5632], P(None, None, 'tp')
- grad_down: float32 [5632, 2048], P('tp')
- grad_gains: float32 [2, 2048], P(None, 'tp')
- grad_biases: float32 [2, 2048], P(None, 'tp')
Inputs may be any that keep to these rules, and one draw needn't show every extreme that they name: `segments`: in each group the ids number the documents from 0 and never fall; every document has 1024 tokens or more.
All inputs are finite; a program needn't handle non-finite values.
Results may differ from a plain program's by a relative error of at most 0.023.
Values may be sent and summed in bfloat16 or wider, within the bound.
A program may use at most 256 MiB of HBM per device.

v0:
```python
import math

import jax
import jax.numpy as jnp
from jax import lax
from jax.sharding import PartitionSpec as P

D = 2048
HEAD_DIM = 64
ROT = 16


EPSILON = 1e-05


def norm_forward(values, gain, shift_bias):
    centre = jnp.mean(values, axis=-1, keepdims=True)
    centred = values - centre
    spread = jnp.mean(centred * centred, axis=-1, keepdims=True)
    inverse = lax.rsqrt(spread + EPSILON)
    normed = centred * inverse
    return (normed * gain + shift_bias, normed, inverse)


def norm_backward(grad_normed, normed, inverse, gain):
    scaled = grad_normed * gain
    inner = jnp.mean(scaled, axis=-1, keepdims=True)
    along = jnp.mean(scaled * normed, axis=-1, keepdims=True)
    return (
        inverse * (scaled - inner - normed * along),
        jnp.sum(grad_normed * normed, axis=0),
        jnp.sum(grad_normed, axis=0),
    )


def rotary_tables(segment_ids):
    places = jnp.arange(segment_ids.shape[0], dtype=jnp.int32)
    starts_here = jnp.concatenate(
        [jnp.ones((1,), dtype=jnp.bool_), segment_ids[1:] != segment_ids[:-1]]
    )
    doc_start = lax.cummax(jnp.where(starts_here, places, 0), axis=0)
    positions = (places - doc_start).astype(jnp.float32)
    halves = ROT // 2
    frequency = jnp.exp(jnp.arange(halves, dtype=jnp.float32) * (-2.0 * math.log(10000.0) / ROT))
    angles = positions[:, None] * frequency[None, :]
    return (jnp.cos(angles)[:, None, :], jnp.sin(angles)[:, None, :])


def rotate(tensor, cosine, sine):
    halves = ROT // 2
    first_half = tensor[..., :halves]
    second_half = tensor[..., halves:ROT]
    return jnp.concatenate(
        [
            first_half * cosine - second_half * sine,
            second_half * cosine + first_half * sine,
            tensor[..., ROT:],
        ],
        axis=-1,
    )


def rotate_back(tensor, cosine, sine):
    halves = ROT // 2
    first_half = tensor[..., :halves]
    second_half = tensor[..., halves:ROT]
    return jnp.concatenate(
        [
            first_half * cosine + second_half * sine,
            second_half * cosine - first_half * sine,
            tensor[..., ROT:],
        ],
        axis=-1,
    )


def contract_rows(left, right):
    return lax.dot_general(
        left, right, (((0,), (0,)), ((), ())), preferred_element_type=jnp.float32
    )


def contract_cols(left, right):
    return lax.dot_general(
        left, right, (((1,), (1,)), ((), ())), preferred_element_type=jnp.float32
    )


def local(
    layer_input,
    segments,
    norm_gains,
    norm_biases,
    w_qkv,
    qv_bias,
    key_bias,
    w_out,
    w_gate_up,
    w_down,
    out_grad,
):
    segment_ids = segments[0]
    group_rows = segment_ids.shape[0]
    local_width = w_qkv.shape[2]
    local_heads = local_width // HEAD_DIM
    local_hidden = w_down.shape[0]
    block_rows = min(512, group_rows)
    blocks = group_rows // block_rows
    scale = HEAD_DIM ** (-0.5)
    places = jnp.arange(group_rows, dtype=jnp.int32)
    cosine, sine = rotary_tables(segment_ids)
    qkv_matrix = w_qkv.reshape(D, 3 * local_width)
    gate_matrix = w_gate_up.reshape(D, 2 * local_hidden)
    x_float = layer_input.astype(jnp.float32)
    normed_one, hat_one, inverse_one = norm_forward(x_float, norm_gains[0], norm_biases[0])
    rows_one = lax.all_gather(normed_one.astype(jnp.bfloat16), "tp", axis=0, tiled=True)
    projected = jnp.dot(rows_one, qkv_matrix, preferred_element_type=jnp.float32).reshape(
        group_rows, 3, local_heads, HEAD_DIM
    )
    key_full = jnp.concatenate(
        [key_bias, jnp.zeros((local_heads, HEAD_DIM - ROT), jnp.float32)], axis=1
    )
    bias_all = jnp.stack(
        [
            qv_bias[0].reshape(local_heads, HEAD_DIM),
            key_full,
            qv_bias[1].reshape(local_heads, HEAD_DIM),
        ]
    )
    projected = projected + bias_all[None]
    queries = rotate(projected[:, 0], cosine, sine).astype(jnp.bfloat16)
    key_rows = rotate(projected[:, 1], cosine, sine).astype(jnp.bfloat16)
    value_rows = projected[:, 2].astype(jnp.bfloat16)
    query_blocks = queries.reshape(blocks, block_rows, local_heads, HEAD_DIM)
    segment_blocks = segment_ids.reshape(blocks, block_rows)
    place_blocks = places.reshape(blocks, block_rows)

    def scores_of(query_block, segment_block, place_block):
        raw = (
            jnp.einsum("bhd,khd->hbk", query_block, key_rows, preferred_element_type=jnp.float32)
            * scale
        )
        visible = (segment_block[:, None] == segment_ids[None, :]) & (
            place_block[:, None] >= places[None, :]
        )
        return jnp.where(visible[None], raw, -jnp.inf)

    def forward_block(item):
        query_block, segment_block, place_block = item
        scores = scores_of(query_block, segment_block, place_block)
        highest = jnp.max(scores, axis=-1, keepdims=True)
        expo = jnp.exp(scores - highest)
        totals = jnp.sum(expo, axis=-1, keepdims=True)
        probs = (expo / totals).astype(jnp.bfloat16)
        mixed = jnp.einsum("hbk,khd->bhd", probs, value_rows, preferred_element_type=jnp.float32)
        return (mixed.astype(jnp.bfloat16), (highest + jnp.log(totals))[..., 0])

    attended, log_totals = lax.map(forward_block, (query_blocks, segment_blocks, place_blocks))
    attended = attended.reshape(group_rows, local_width)
    hidden_state = x_float + lax.psum_scatter(
        jnp.dot(attended, w_out, preferred_element_type=jnp.float32).astype(jnp.bfloat16),
        "tp",
        scatter_dimension=0,
        tiled=True,
    ).astype(jnp.float32)
    normed_two, hat_two, inverse_two = norm_forward(hidden_state, norm_gains[1], norm_biases[1])
    rows_two = lax.all_gather(normed_two.astype(jnp.bfloat16), "tp", axis=0, tiled=True)
    gate_up = jnp.dot(rows_two, gate_matrix, preferred_element_type=jnp.float32).reshape(
        group_rows, 2, local_hidden
    )
    gate_part = gate_up[:, 0]
    up_part = gate_up[:, 1]
    sigmoid_gate = jax.nn.sigmoid(gate_part)
    silu_gate = gate_part * sigmoid_gate
    activation = (silu_gate * up_part).astype(jnp.bfloat16)
    output = hidden_state + lax.psum_scatter(
        jnp.dot(activation, w_down, preferred_element_type=jnp.float32).astype(jnp.bfloat16),
        "tp",
        scatter_dimension=0,
        tiled=True,
    ).astype(jnp.float32)
    grad_float = out_grad.astype(jnp.float32)
    portion = lax.all_gather(out_grad, "tp", axis=0, tiled=True)
    weight_sum = contract_rows(activation, portion)
    grad_act = contract_cols(portion, w_down)
    grad_down, grad_act = (weight_sum, grad_act)
    grad_gate = grad_act * up_part * sigmoid_gate * (1.0 + gate_part * (1.0 - sigmoid_gate))
    grad_up = grad_act * silu_gate
    grad_pair = (
        jnp.stack([grad_gate, grad_up], axis=1)
        .astype(jnp.bfloat16)
        .reshape(group_rows, 2 * local_hidden)
    )
    grad_gate_up = contract_rows(rows_two, grad_pair).reshape(D, 2, local_hidden)
    grad_normed_two = lax.psum_scatter(
        contract_cols(grad_pair, gate_matrix).astype(jnp.bfloat16),
        "tp",
        scatter_dimension=0,
        tiled=True,
    ).astype(jnp.float32)
    back_two, gain_two, shift_two = norm_backward(
        grad_normed_two, hat_two, inverse_two, norm_gains[1]
    )
    grad_hidden = grad_float + back_two
    portion = lax.all_gather(grad_hidden.astype(jnp.bfloat16), "tp", axis=0, tiled=True)
    weight_sum = contract_rows(attended, portion)
    grad_att = contract_cols(portion, w_out)
    grad_out = weight_sum
    grad_blocks = grad_att.astype(jnp.bfloat16).reshape(blocks, block_rows, local_heads, HEAD_DIM)

    def backward_block(running, item):
        grad_keys, grad_values = running
        query_block, grad_block, log_block, segment_block, place_block = item
        scores = scores_of(query_block, segment_block, place_block)
        weights = jnp.exp(scores - log_block[..., None])
        grad_values = grad_values + jnp.einsum(
            "hbk,bhd->khd",
            weights.astype(jnp.bfloat16),
            grad_block,
            preferred_element_type=jnp.float32,
        )
        grad_weights = jnp.einsum(
            "bhd,khd->hbk", grad_block, value_rows, preferred_element_type=jnp.float32
        )
        inner = jnp.sum(weights * grad_weights, axis=-1, keepdims=True)
        grad_scores = (weights * (grad_weights - inner)).astype(jnp.bfloat16)
        grad_query = (
            jnp.einsum("hbk,khd->bhd", grad_scores, key_rows, preferred_element_type=jnp.float32)
            * scale
        )
        grad_keys = (
            grad_keys
            + jnp.einsum(
                "hbk,bhd->khd", grad_scores, query_block, preferred_element_type=jnp.float32
            )
            * scale
        )
        return ((grad_keys, grad_values), grad_query)

    zero_heads = jnp.zeros((group_rows, local_heads, HEAD_DIM), jnp.float32)
    (grad_keys, grad_values), grad_queries = lax.scan(
        backward_block,
        (zero_heads, zero_heads),
        (query_blocks, grad_blocks, log_totals, segment_blocks, place_blocks),
    )
    grad_queries = grad_queries.reshape(group_rows, local_heads, HEAD_DIM)
    grad_projected = jnp.stack(
        [
            rotate_back(grad_queries, cosine, sine),
            rotate_back(grad_keys, cosine, sine),
            grad_values,
        ],
        axis=1,
    ).astype(jnp.bfloat16)
    bias_sums = jnp.sum(grad_projected, axis=0, dtype=jnp.float32)
    grad_qv = jnp.stack([bias_sums[0].reshape(local_width), bias_sums[2].reshape(local_width)])
    grad_key = bias_sums[1][:, :ROT]
    grad_flat = grad_projected.reshape(group_rows, 3 * local_width)
    grad_qkv = contract_rows(rows_one, grad_flat).reshape(D, 3, local_width)
    grad_normed_one = lax.psum_scatter(
        contract_cols(grad_flat, qkv_matrix).astype(jnp.bfloat16),
        "tp",
        scatter_dimension=0,
        tiled=True,
    ).astype(jnp.float32)
    back_one, gain_one, shift_one = norm_backward(
        grad_normed_one, hat_one, inverse_one, norm_gains[0]
    )
    grad_input = grad_hidden + back_one
    gain_grads, shift_grads = (
        lax.psum_scatter(
            jnp.stack([gain_one, gain_two]).astype(jnp.bfloat16),
            "tp",
            scatter_dimension=1,
            tiled=True,
        ).astype(jnp.float32),
        lax.psum_scatter(
            jnp.stack([shift_one, shift_two]).astype(jnp.bfloat16),
            "tp",
            scatter_dimension=1,
            tiled=True,
        ).astype(jnp.float32),
    )
    grad_qkv, grad_qv, grad_key, grad_out, grad_gate_up, grad_down, gain_grads, shift_grads = (
        lax.psum(grad_qkv.astype(jnp.bfloat16), "dp").astype(jnp.float32),
        lax.psum(grad_qv.astype(jnp.bfloat16), "dp").astype(jnp.float32),
        lax.psum(grad_key.astype(jnp.bfloat16), "dp").astype(jnp.float32),
        lax.psum(grad_out.astype(jnp.bfloat16), "dp").astype(jnp.float32),
        lax.psum(grad_gate_up.astype(jnp.bfloat16), "dp").astype(jnp.float32),
        lax.psum(grad_down.astype(jnp.bfloat16), "dp").astype(jnp.float32),
        lax.psum(gain_grads.astype(jnp.bfloat16), "dp").astype(jnp.float32),
        lax.psum(shift_grads.astype(jnp.bfloat16), "dp").astype(jnp.float32),
    )
    return (
        output,
        grad_input,
        grad_qkv,
        grad_qv,
        grad_key,
        grad_out,
        grad_gate_up,
        grad_down,
        gain_grads,
        shift_grads,
    )


def solution(mesh):
    in_specs = (
        P(("dp", "tp"), None),
        P("dp", None),
        P(),
        P(),
        P(None, None, "tp"),
        P(None, "tp"),
        P("tp", None),
        P("tp", None),
        P(None, None, "tp"),
        P("tp", None),
        P(("dp", "tp"), None),
    )
    out_specs = (
        P(("dp", "tp"), None),
        P(("dp", "tp"), None),
        P(None, None, "tp"),
        P(None, "tp"),
        P("tp", None),
        P("tp", None),
        P(None, None, "tp"),
        P("tp", None),
        P(None, "tp"),
        P(None, "tp"),
    )
    return jax.shard_map(local, mesh=mesh, in_specs=in_specs, out_specs=out_specs, check_vma=False)
```

profile of v0, /device:TPU:0, one launch (start us, length us, event | category | flops | bytes accessed | tf_op | source)
XLA Modules:
  0.0 1481.0 jit_solution(10848038059797148822)
XLA Ops:
  18.1 4.6 copy.36
  23.3 49.9 %all-gather.5.cloned.1.call-done = bf16[2048,2048]{1,0:T(8,128)(2,1)} async-done(((bf16[256,2048]{1,0:T(8,128)(2,1)}), bf16[2048,2048]{1,0:T(8,128)(2,1)}) %all-gather.5.cloned.1.call-update) | async-done | bytes 8388624 | tf_op jit(solution)/shard_map/all_gather | solution.py:116
  73.2 10.1 fusion.63
  88.5 64.2 %while.28 = (s32[]{:T(128)}, bf16[4,512,4,64]{1,3,2,0:T(8,128)(2,1)}, f32[4,4,512]{2,1,0:T(4,128)S(1)}, s32[4,512]{1,0:T(4,128)S(1)}, s32[1,2048]{1,0:T(1,128)S(...) while((s32[]{:T(128)}, ...), condition=%wide.region_7.8_spmd.clone, body=%wide.region_4.7_spmd.clone.sunk | while | flops 1127348224 | bytes 61427864 | solution.py:158
  89.7 4.4 fusion.148
  94.2 4.3 fusion.149
  98.5 5.9 fusion.150
  105.6 4.4 fusion.148
  110.1 4.3 fusion.149
  114.4 5.9 fusion.150
  121.6 4.4 fusion.148
  126.0 4.3 fusion.149
  130.3 5.9 fusion.150
  137.5 4.4 fusion.148
  141.9 4.3 fusion.149
  146.3 5.9 fusion.150
  156.1 5.8 convolution_convert_fusion.2
  162.0 71.6 %reduce-scatter.11.cloned.1.call-done = bf16[256,2048]{1,0:T(8,128)(2,1)} async-done(((bf16[2048,2048]{1,0:T(8,128)(2,1)}), bf16[256,2048]{1,0:T(8,128)(2,1)}) %reduce-scatter.11.cloned.1.call-update) | async-done | bytes 1048592 | tf_op jit(solution)/shard_map/reduce_scatter | solution.py:160
  239.9 53.8 %all-gather.7.cloned.1.call-done = bf16[2048,2048]{1,0:T(8,128)(2,1)} async-done(((bf16[256,2048]{1,0:T(8,128)(2,1)}), bf16[2048,2048]{1,0:T(8,128)(2,1)}) %all-gather.7.cloned.1.call-update) | async-done | bytes 8388624 | tf_op jit(solution)/shard_map/all_gather | solution.py:167
  293.7 18.8 %fusion.53 = f32[2048,2,704]{0,2,1:T(8,128)} fusion(bf16[2048,2048]{1,0:T(8,128)(2,1)} %all-gather.7.cloned.1.call-done, bf16[2048,2,704]{0,2,1:T(8,128)(2,1)} %param.23), kind=kOutput, calls=%fused_computation.64 | convolution fusion | flops 11811160064 | bytes 25690112 | tf_op jit(solution)/shard_map/dot_general | solution.py:168
  312.5 37.2 %all-gather.9.cloned.1.call-done = bf16[2048,2048]{1,0:T(8,128)(2,1)} async-done(((bf16[256,2048]{1,0:T(8,128)(2,1)}), bf16[2048,2048]{1,0:T(8,128)(2,1)}) %all-gather.9.cloned.1.call-update) | async-done | bytes 8388624 | tf_op jit(solution)/shard_map/all_gather | solution.py:183
  349.7 12.9 multiply_bitcast_fusion.1
  365.2 17.6 %bitcast_convert_fusion = bf16[2048,2048]{1,0:T(8,128)(2,1)} fusion(bf16[2048,2,704]{0,2,1:T(8,128)(2,1)} %param.23, bf16[2048,1,704]{0,2,1:T(8,128)(2,1)S(1)} %get-tuple-element.303, bf16[2048,1,704]{0,2,1:T(8,128)(2,1)S(1)} %get-tuple-element.302), kind=kOutput, calls=%fused_computation.56 | convolution fusion | flops 11818237952 | bytes 19922944 | tf_op jit(solution)/shard_map/dot_general | solution.py:84
  382.9 71.6 %reduce-scatter.15.cloned.1.call-done = bf16[256,2048]{1,0:T(8,128)(2,1)} async-done(((bf16[2048,2048]{1,0:T(8,128)(2,1)}), bf16[256,2048]{1,0:T(8,128)(2,1)}) %reduce-scatter.15.cloned.1.call-update) | async-done | bytes 1048592 | tf_op jit(solution)/shard_map/reduce_scatter | solution.py:195
  461.7 54.3 %all-gather.11.cloned.1.call-done = bf16[2048,2048]{1,0:T(8,128)(2,1)} async-done(((bf16[256,2048]{1,0:T(8,128)(2,1)}), bf16[2048,2048]{1,0:T(8,128)(2,1)}) %all-gather.11.cloned.1.call-update) | async-done | bytes 8388624 | tf_op jit(solution)/shard_map/all_gather | solution.py:205
  516.0 7.0 convolution_convert_fusion.5
  523.0 4.4 reshape.363
  527.4 4.0 copy.42
  531.4 246.2 %while.29 = (s32[]{:T(128)}, f32[2048,4,64]{0,2,1:T(8,128)}, f32[2048,4,64]{0,2,1:T(8,128)}, f32[4,512,4,64]{1,0,3,2:T(4,128)}, bf16[4,512,4,64]{1,3,2,0:T(8,128...) while((s32[]{:T(128)}, f32[2048,4,64]{0,2,1:T(8,128)}, ...), condition=%wide.region_17.18_spmd.clone, body=%wide.region_15.17_spmd.clone.sunk | while | flops 2753165312 | bytes 233386272 | solution.py:241
  536.6 5.7 copy-done.1
  542.3 7.1 fusion.163
  549.4 12.8 multiply_reduce_fusion.3
  562.2 12.2 multiply_convert_fusion.3
  581.6 11.1 dynamic_update_slice.22
  597.7 5.7 copy-done.1
  603.4 7.5 fusion.163
  610.9 12.8 multiply_reduce_fusion.3
  623.7 12.2 multiply_convert_fusion.3
  643.1 11.1 dynamic_update_slice.22
  659.2 5.7 copy-done.1
  664.9 7.5 fusion.163
  672.4 12.8 multiply_reduce_fusion.3
  685.2 12.2 multiply_convert_fusion.3
  704.6 11.1 dynamic_update_slice.22
  720.7 5.7 copy-done.1
  726.4 7.5 fusion.163
  733.9 12.8 multiply_reduce_fusion.3
  746.7 12.2 multiply_convert_fusion.3
  766.1 11.1 dynamic_update_slice.22
  788.9 9.2 convolution_convert_fusion
  798.1 5.3 multiply_convert_fusion.1
  805.0 9.1 convolution_convert_fusion.1
  814.1 11.0 convolution_convert_fusion.3
  825.2 16.2 %fusion.58 = bf16[2048,2,704]{0,2,1:T(8,128)(2,1)} fusion(bf16[2048,2048]{1,0:T(8,128)(2,1)} %all-gather.7.cloned.1.call-done, bf16[2048,1,704]{0,2,1:T(8,128)(2,1)S(1)} %copy-done.47, bf16[2048,1,704]{0,2,1:T(8,128)(2,1)S(1)} %copy-done.45), kind=kOutput, calls=%fused_computation.79 | convolution fusion | flops 11825577984 | bytes 19922944 | tf_op jit(solution)/shard_map/dot_general | solution.py:78
  842.9 11.7 fusion.66
  854.5 15.2 %reduce-scatter.17.cloned.1.call-done = bf16[256,2048]{1,0:T(8,128)(2,1)} async-done(((bf16[2048,2048]{1,0:T(8,128)(2,1)}), bf16[256,2048]{1,0:T(8,128)(2,1)}) %reduce-scatter.17.cloned.1.call-update) | async-done | bytes 1048592 | tf_op jit(solution)/shard_map/reduce_scatter | solution.py:260
  876.0 7.5 convolution_convert_fusion.4
  883.8 61.5 %reduce-scatter.13.cloned.1.call-done = bf16[256,2048]{1,0:T(8,128)(2,1)} async-done(((bf16[2048,2048]{1,0:T(8,128)(2,1)}), bf16[256,2048]{1,0:T(8,128)(2,1)}) %reduce-scatter.13.cloned.1.call-update) | async-done | bytes 1048592 | tf_op jit(solution)/shard_map/reduce_scatter | solution.py:176
  945.3 5.3 fusion.83
  950.6 32.5 %reduce-scatter.19.cloned.1.call-done = bf16[256,2]{1,0:T(8,128)(2,1)} async-done(((bf16[2048,2]{1,0:T(8,128)(2,1)}), bf16[256,2]{1,0:T(8,128)(2,1)}) %reduce-scatter.19.cloned.1.call-update) | async-done | bytes 1040
  984.0 36.2 %reduce-scatter.21.cloned.1.call-done = bf16[256,2]{1,0:T(8,128)(2,1)} async-done(((bf16[2048,2]{1,0:T(8,128)(2,1)}), bf16[256,2]{1,0:T(8,128)(2,1)}) %reduce-scatter.21.cloned.1.call-update) | async-done | bytes 1040
  1021.1 11.9 all-reduce.1
  1035.3 423.0 %all-reduce.5.cloned.1.call-done = (bf16[2048,3,256]{2,0,1:T(8,128)(2,1)}, bf16[256,2048]{1,0:T(8,128)(2,1)}, bf16[2048,2,704]{0,2,1:T(8,128)(2,1)}, bf16[704,2048]{1,0:T(8,128)(2,1)}) async-done(((bf16[2048,3,256]{2,0,1:T(8,128)(2,1)}, bf16[256,2048]{1,0:T(8,128)(2,1)}, bf16[2048,2,704]{0,2,1:T(8,128)(2,1)}, bf16[704,2048]{1,0:T(8,128)(2,1)}), (bf16[2048,3,256]{2,0,1:T(8,128)(2,1)}, ...) | async-done | bytes 12845072 | tf_op jit(solution)/shard_map/psum | solution.py:285
  1468.3 6.0 convert_element_type.171
  (271 shorter events, 124.2 us)
Async XLA Ops:
  7.2 342.6 %copy-start = (bf16[704,2048]{1,0:T(8,128)(2,1)S(1)}, bf16[704,2048]{1,0:T(8,128)(2,1)}, u32[]{:S(2)}) copy-start(bf16[704,2048]{1,0:T(8,128)(2,1)} %param.24) | copy-start | bytes 8650756
  7.2 8.9 copy-start.42
  7.2 9.6 copy-start.18
  7.2 66.0 %all-gather.5.cloned.1.call-start = ((), (), s32[]{:S(2)}) async-start(), calls=%async_computation.6 | async-start | bytes 9437184 | tf_op jit(solution)/shard_map/all_gather | solution.py:116
  8.9 4.5 copy-start.31
  10.5 2.8 copy-start.35
  16.0 217.5 %reduce-scatter.11.cloned.1.call-start = ((), (), s32[]{:S(2)}) async-start(), calls=%async_computation.7 | async-start | bytes 9437184 | tf_op jit(solution)/shard_map/reduce_scatter | solution.py:160
  18.1 4.7 copy-start.43
  23.3 61.6 %copy-start.20 = (f32[2048,8]{0,1:T(8,128)}, f32[2048,8]{0,1:T(8,128)S(1)}, u32[]{:S(2)}) copy-start(f32[2048,8]{0,1:T(8,128)S(1)} %get-tuple-element.324) | copy-start | bytes 196612
  23.3 61.6 %copy-start.22 = (f32[2048,8]{0,1:T(8,128)}, f32[2048,8]{0,1:T(8,128)S(1)}, u32[]{:S(2)}) copy-start(f32[2048,8]{0,1:T(8,128)S(1)} %get-tuple-element.325) | copy-start | bytes 196612
  94.1 4.3 copy-start.7
  110.1 4.3 copy-start.7
  126.0 4.3 copy-start.7
  141.9 4.3 copy-start.7
  152.7 3.4 copy-start.19
  161.9 75.8 %copy-start.24 = (f32[1,2048]{1,0:T(1,128)S(1)}, f32[1,2048]{1,0:T(1,128)}, u32[]{:S(2)}) copy-start(f32[1,2048]{1,0:T(1,128)} %get-tuple-element.321) | copy-start | bytes 24580
  161.9 75.8 %copy-start.30 = (f32[1,2048]{1,0:T(1,128)S(1)}, f32[1,2048]{1,0:T(1,128)}, u32[]{:S(2)}) copy-start(f32[1,2048]{1,0:T(1,128)} %get-tuple-element.323) | copy-start | bytes 24580
  161.9 131.8 %all-gather.7.cloned.1.call-start = ((), (), s32[]{:S(2)}) async-start(), calls=%async_computation.8 | async-start | bytes 9437184 | tf_op jit(solution)/shard_map/all_gather | solution.py:167
  233.6 4.1 copy-start.3
  233.6 4.2 copy-start.8
  235.6 222.5 %copy-start.28 = (f32[256]{0:T(256)}, f32[256]{0:T(256)S(1)}, u32[]{:S(2)}) copy-start(f32[256]{0:T(256)S(1)} %broadcast_multiply_fusion.4) | copy-start | bytes 3076
  237.7 220.5 %copy-start.33 = (f32[256]{0:T(256)}, f32[256]{0:T(256)S(1)}, u32[]{:S(2)}) copy-start(f32[256]{0:T(256)S(1)} %add_rsqrt_fusion) | copy-start | bytes 3076
  239.3 110.5 %all-gather.9.cloned.1.call-start = ((), (), s32[]{:S(2)}) async-start(), calls=%async_computation.10 | async-start | bytes 9437184 | tf_op jit(solution)/shard_map/all_gather | solution.py:183
  239.9 214.6 %reduce-scatter.15.cloned.1.call-start = ((), (), s32[]{:S(2)}) async-start(), calls=%async_computation.11 | async-start | bytes 9437184 | tf_op jit(solution)/shard_map/reduce_scatter | solution.py:195
  382.8 133.2 %all-gather.11.cloned.1.call-start = ((), (), s32[]{:S(2)}) async-start(), calls=%async_computation.12 | async-start | bytes 9437184 | tf_op jit(solution)/shard_map/all_gather | solution.py:205
  454.5 3.7 copy-start.4
  454.5 3.7 copy-start.9
  454.5 3.7 copy-start.10
  458.1 3.5 copy-start.38
  458.1 3.5 copy-start.40
  461.6 408.1 %reduce-scatter.17.cloned.1.call-start = ((), (), s32[]{:S(2)}) async-start(), calls=%async_computation.13 | async-start | bytes 9437184 | tf_op jit(solution)/shard_map/reduce_scatter | solution.py:260
  536.6 5.7 copy-start.1
  562.2 12.2 copy-start.2
  574.4 2.7 copy-start.5
  597.7 5.7 copy-start.1
  623.7 12.2 copy-start.2
  635.9 2.7 copy-start.5
  659.2 5.7 copy-start.1
  685.2 12.2 copy-start.2
  697.4 2.7 copy-start.5
  720.7 5.7 copy-start.1
  746.7 12.2 copy-start.2
  758.9 2.7 copy-start.5
  777.6 5.2 copy-start.21
  777.6 5.2 copy-start.23
  798.1 147.2 %reduce-scatter.13.cloned.1.call-start = ((), (), s32[]{:S(2)}) async-start(), calls=%async_computation.9 | async-start | bytes 9437184 | tf_op jit(solution)/shard_map/reduce_scatter | solution.py:176
  814.0 169.1 %reduce-scatter.19.cloned.1.call-start = ((), (), s32[]{:S(2)}) async-start(), calls=%async_computation.14 | async-start | bytes 589824
  814.1 11.1 copy-start.45
  814.1 11.0 copy-start.47
  825.1 17.7 %copy-start.37 = (bf16[2048]{0:T(1024)(128)(2,1)S(1)}, bf16[2048]{0:T(1024)(128)(2,1)}, u32[]{:S(2)}) copy-start(bf16[2048]{0:T(1024)(128)(2,1)} %get-tuple-element.234) | copy-start | bytes 12292
  842.8 28.3 %copy-start.27 = (f32[1,2048]{1,0:T(1,128)S(1)}, f32[1,2048]{1,0:T(1,128)}, u32[]{:S(2)}) copy-start(f32[1,2048]{1,0:T(1,128)} %copy-done.26) | copy-start | bytes 24580
  842.8 28.3 %copy-start.32 = (f32[256]{0:T(256)S(1)}, f32[256]{0:T(256)}, u32[]{:S(2)}) copy-start(f32[256]{0:T(256)} %copy-done.31) | copy-start | bytes 3076
  842.8 28.3 %copy-start.36 = (f32[256]{0:T(256)S(1)}, f32[256]{0:T(256)}, u32[]{:S(2)}) copy-start(f32[256]{0:T(256)} %copy-done.35) | copy-start | bytes 3076
  874.8 145.4 %reduce-scatter.21.cloned.1.call-start = ((), (), s32[]{:S(2)}) async-start(), calls=%async_computation.15 | async-start | bytes 589824
  875.9 582.3 %all-reduce.5.cloned.1.call-start = ((), (), s32[]{:S(2)}) async-start(), calls=%async_computation.16 | async-start | bytes 25690112 | tf_op jit(solution)/shard_map/psum | solution.py:285
  883.5 61.7 %copy-start.25 = (f32[1,2048]{1,0:T(1,128)S(1)}, f32[1,2048]{1,0:T(1,128)}, u32[]{:S(2)}) copy-start(f32[1,2048]{1,0:T(1,128)} %get-tuple-element.321) | copy-start | bytes 24580
  883.5 61.7 %copy-start.29 = (f32[256]{0:T(256)S(1)}, f32[256]{0:T(256)}, u32[]{:S(2)}) copy-start(f32[256]{0:T(256)} %copy-done.28) | copy-start | bytes 3076
  883.5 61.7 %copy-start.34 = (f32[256]{0:T(256)S(1)}, f32[256]{0:T(256)}, u32[]{:S(2)}) copy-start(f32[256]{0:T(256)} %copy-done.33) | copy-start | bytes 3076
  883.5 61.8 %copy-start.39 = (f32[256]{0:T(256)S(1)}, f32[256]{0:T(256)}, u32[]{:S(2)}) copy-start(f32[256]{0:T(256)} %copy-done.38) | copy-start | bytes 3076
  883.5 61.7 %copy-start.41 = (f32[256]{0:T(256)S(1)}, f32[256]{0:T(256)}, u32[]{:S(2)}) copy-start(f32[256]{0:T(256)} %copy-done.40) | copy-start | bytes 3076
  1458.3 2.9 copy-start.14
  1458.3 10.0 slice-start
  1461.2 3.7 copy-start.16
  1461.2 7.1 slice-start.1
  (12 other events, 19.8 us)
Sparse Core Ops, SparseCore 0:
  16.2 56.9 all-gather.4
  162.0 71.4 reduce-scatter.10
  239.4 54.2 all-gather.6
  295.4 54.2 all-gather.8
  382.9 71.4 reduce-scatter.14
  461.7 54.2 all-gather.10
  798.2 71.4 reduce-scatter.16
  873.7 71.4 reduce-scatter.12
  948.9 34.1 reduce-scatter.18
  986.0 34.1 reduce-scatter.20
  1023.6 434.6 all-reduce.4
where the time goes:
time: 1490 us; the launch traced here: 1480 us
  waiting for transfers between devices  907 us (61%)
  matrix products  295 us (20%)
  other arithmetic  133 us (9%)
  local copies, waits for them, and re-layouts  116 us (8%)
    psum x1, waiting for transfers between devices, local(): lax.psum(grad_qkv.astype(jnp.bfloat16), 'dp').astype(jnp.float32)  423 us
    reduce_scatter x1, waiting for transfers between devices, local(): lax.psum_scatter(contract_cols(grad_pair, gate_matrix).astype(jnp.bfloat1...  71.6 us
    reduce_scatter x1, waiting for transfers between devices, local(): lax.psum_scatter(jnp.dot(attended, w_out, preferred_element_type=jnp.floa...  71.6 us
    unnamed x13, waiting for transfers between devices  69.3 us
    reduce_scatter x1, waiting for transfers between devices, local(): lax.psum_scatter(jnp.dot(activation, w_down, preferred_element_type=jnp.f...  61.5 us
    all_gather x1, waiting for transfers between devices, local(): lax.all_gather(grad_hidden.astype(jnp.bfloat16), 'tp', axis=0, tiled=True)  54.3 us
    all_gather x1, waiting for transfers between devices, local(): lax.all_gather(normed_two.astype(jnp.bfloat16), 'tp', axis=0, tiled=True)  53.8 us
    dot_general x4, matrix products, backward_block(): jnp.einsum('bhd,khd->hbk', grad_block, value_rows, preferred_element_type...  51.2 us
  transfers between devices with their start and end apart: 11, of which 11 were waited for; matrix products, arithmetic and copies ran while one was open for 7% of the time, Pallas kernels for 0%

commit v1 on v0

v1 whole, which is shorter than its diff:
```python
import functools
import math

import jax
import jax.numpy as jnp
from jax import lax
from jax.experimental import pallas as pl
from jax.experimental.pallas import tpu as pltpu
from jax.sharding import PartitionSpec as P

D = 2048
HEAD_DIM = 64
ROT = 16
EPSILON = 1e-05
MESH = pl.DeviceIdType.MESH
NT = (((1,), (1,)), ((), ()))
TN = (((0,), (0,)), ((), ()))


def norm_forward(values, gain, shift_bias):
    centre = jnp.mean(values, axis=-1, keepdims=True)
    centred = values - centre
    spread = jnp.mean(centred * centred, axis=-1, keepdims=True)
    inverse = lax.rsqrt(spread + EPSILON)
    normed = centred * inverse
    return (normed * gain + shift_bias, normed, inverse)


def norm_backward(grad_normed, normed, inverse, gain):
    scaled = grad_normed * gain
    inner = jnp.mean(scaled, axis=-1, keepdims=True)
    along = jnp.mean(scaled * normed, axis=-1, keepdims=True)
    return (
        inverse * (scaled - inner - normed * along),
        jnp.sum(grad_normed * normed, axis=0),
        jnp.sum(grad_normed, axis=0),
    )


def contract_rows(left, right):
    return lax.dot_general(left, right, TN, preferred_element_type=jnp.float32)


def contract_cols(left, right):
    return lax.dot_general(left, right, NT, preferred_element_type=jnp.float32)


def whole(shape):
    return pl.BlockSpec(shape, lambda step: (0,) * len(shape))


def turn(values, table, flip, lane):
    width = values.shape[1]
    ahead = pltpu.roll(values, width - ROT // 2, 1)
    behind = pltpu.roll(values, ROT // 2, 1)
    return values * table + jnp.where(lane < ROT // 2, ahead, behind) * flip


def rotary_tables(segment_ids):
    places = jnp.arange(segment_ids.shape[0], dtype=jnp.int32)
    fresh = jnp.concatenate([jnp.ones((1,), jnp.bool_), segment_ids[1:] != segment_ids[:-1]])
    starts = lax.cummax(jnp.where(fresh, places, 0), axis=0)
    halves = ROT // 2
    lane = jnp.arange(128, dtype=jnp.int32) % HEAD_DIM
    frequency = jnp.exp((lane % halves).astype(jnp.float32) * (-2.0 * math.log(10000.0) / ROT))
    frequency = jnp.where(lane < ROT, frequency, 0.0)
    angles = (places - starts).astype(jnp.float32)[:, None] * frequency[None, :]
    sign = jnp.where(lane < halves, -1.0, 1.0).astype(jnp.float32)
    return jnp.cos(angles), jnp.sin(angles) * sign[None, :], starts


def project_kernel(x_ref, w_ref, bias_ref, cos_ref, sin_ref, q_ref, k_ref, v_ref):
    width = q_ref.shape[1]
    value = jnp.dot(x_ref[...], w_ref[...], preferred_element_type=jnp.float32) + bias_ref[:1, :]
    lane = lax.broadcasted_iota(jnp.int32, (1, width), 1) % HEAD_DIM
    table = jnp.tile(cos_ref[...], (1, width // 128))
    flip = jnp.tile(sin_ref[...], (1, width // 128))
    q_ref[...] = turn(value[:, :width], table, flip, lane).astype(jnp.bfloat16)
    k_ref[...] = turn(value[:, width:2 * width], table, flip, lane).astype(jnp.bfloat16)
    v_ref[...] = value[:, 2 * width:].astype(jnp.bfloat16)


def project(x, w, bias, cos, sin):
    rows = x.shape[0]
    width = w.shape[1] // 3
    block = min(512, rows)
    tall = lambda cols: pl.BlockSpec((block, cols), lambda step: (step, 0))
    return pl.pallas_call(
        project_kernel,
        grid=(rows // block,),
        in_specs=[tall(D), whole(w.shape), whole(bias.shape), tall(128), tall(128)],
        out_specs=[tall(width)] * 3,
        out_shape=[jax.ShapeDtypeStruct((rows, width), jnp.bfloat16)] * 3,
        cost_estimate=pl.CostEstimate(flops=2 * rows * D * 3 * width, bytes_accessed=2 * rows * D + 12 * D * width, transcendentals=0),
        name="project",
    )(x, w, bias, cos, sin)


def forward_kernel(block, q_ref, k_ref, v_ref, start_ref, out_ref, lse_ref):
    head = pl.program_id(0)
    rows, width = q_ref.shape
    own = lax.broadcasted_iota(jnp.int32, (1, width), 1) // HEAD_DIM == head
    for index in range(rows // block):
        low, high = index * block, (index + 1) * block
        query = jnp.where(own, q_ref[low:high, :] * jnp.bfloat16(HEAD_DIM**-0.5), jnp.bfloat16(0))
        scores = lax.dot_general(query, k_ref[:high, :], NT, preferred_element_type=jnp.float32)
        key_place = lax.broadcasted_iota(jnp.int32, (block, high), 1)
        place = low + lax.broadcasted_iota(jnp.int32, (block, high), 0)
        seen = (key_place >= start_ref[low:high, :1]) & (key_place <= place)
        scores = jnp.where(seen, scores, -jnp.inf)
        top = jnp.max(scores, axis=1, keepdims=True)
        expo = jnp.exp(scores - top)
        total = jnp.sum(expo, axis=1, keepdims=True)
        mixed = jnp.dot(expo.astype(jnp.bfloat16), v_ref[:high, :], preferred_element_type=jnp.float32)
        mixed = (mixed / total).astype(jnp.bfloat16)

        @pl.when(head == 0)
        def _():
            out_ref[low:high, :] = mixed

        @pl.when(head > 0)
        def _():
            out_ref[low:high, :] = jnp.where(own, mixed, out_ref[low:high, :])

        spread = jnp.broadcast_to(top + jnp.log(total), (block, 128))
        lse_ref[0, :, low:high] = jnp.transpose(spread)[:8, :]


def attention_forward(q, k, v, start, block=256):
    rows, width = q.shape
    heads = width // HEAD_DIM
    return pl.pallas_call(
        functools.partial(forward_kernel, block),
        grid=(heads,),
        in_specs=[whole((rows, width))] * 3 + [whole((rows, 128))],
        out_specs=[whole((rows, width)), pl.BlockSpec((1, 8, rows), lambda step: (step, 0, 0))],
        out_shape=[
            jax.ShapeDtypeStruct((rows, width), jnp.bfloat16),
            jax.ShapeDtypeStruct((heads, 8, rows), jnp.float32),
        ],
        cost_estimate=pl.CostEstimate(flops=8 * rows * rows * width, bytes_accessed=12 * rows * width, transcendentals=rows * rows * heads // 2),
        name="attention_forward",
    )(q, k, v, start)


def backward_kernel(
    block, q_ref, k_ref, v_ref, o_ref, g_ref, lse_ref, start_ref, cos_ref, sin_ref, out_ref, sums_ref, dq, dk, dv, delta
):
    head = pl.program_id(0)
    rows, width = q_ref.shape
    heads = width // HEAD_DIM
    own = lax.broadcasted_iota(jnp.int32, (1, width), 1) // HEAD_DIM == head

    @pl.when(head == 0)
    def _():
        dq[...] = jnp.zeros_like(dq)
        dk[...] = jnp.zeros_like(dk)
        dv[...] = jnp.zeros_like(dv)

    pick = (own & (lax.broadcasted_iota(jnp.int32, (8, width), 0) >= 0)).astype(jnp.float32)
    product = g_ref[...].astype(jnp.float32) * o_ref[...].astype(jnp.float32)
    delta[...] = lax.dot_general(pick, product, NT, precision=lax.Precision.HIGHEST, preferred_element_type=jnp.float32)
    zero = jnp.bfloat16(0)
    for index in range(rows // block):
        low, high = index * block, (index + 1) * block
        span = rows - low
        key = jnp.where(own, k_ref[low:high, :], zero)
        value = jnp.where(own, v_ref[low:high, :], zero)
        query = q_ref[low:, :]
        grad = g_ref[low:, :]
        scores = lax.dot_general(key * jnp.bfloat16(HEAD_DIM**-0.5), query, NT, preferred_element_type=jnp.float32)
        key_place = low + lax.broadcasted_iota(jnp.int32, (block, span), 0)
        place = low + lax.broadcasted_iota(jnp.int32, (block, span), 1)
        seen = (key_place >= start_ref[:1, low:]) & (key_place <= place)
        weights = jnp.exp(jnp.where(seen, scores, -jnp.inf) - lse_ref[0, :1, low:])
        grad_probs = lax.dot_general(value, grad, NT, preferred_element_type=jnp.float32)
        grad_scores = (weights * (grad_probs - delta[:1, low:])).astype(jnp.bfloat16)
        probs = weights.astype(jnp.bfloat16)
        dv[low:high, :] += jnp.where(own, jnp.dot(probs, grad, preferred_element_type=jnp.float32), 0.0)
        dk[low:high, :] += jnp.where(own, jnp.dot(grad_scores, query, preferred_element_type=jnp.float32), 0.0)
        dq[low:, :] += lax.dot_general(grad_scores, key, TN, preferred_element_type=jnp.float32)

    @pl.when(head == heads - 1)
    def _():
        lane = lax.broadcasted_iota(jnp.int32, (1, width), 1) % HEAD_DIM
        step = min(256, rows)
        sums_ref[...] = jnp.zeros_like(sums_ref)

        @pl.loop(0, rows // step)
        def _(index):
            here = pl.ds(pl.multiple_of(index * step, step), step)
            table = jnp.tile(cos_ref[here, :], (1, width // 128))
            flip = -jnp.tile(sin_ref[here, :], (1, width // 128))
            for part, source in enumerate((dq, dk, dv)):
                value = source[here, :]
                if part < 2:
                    value = turn(value * HEAD_DIM**-0.5, table, flip, lane)
                value = value.astype(jnp.bfloat16)
                columns = slice(part * width, (part + 1) * width)
                out_ref[here, columns] = value
                total = jnp.sum(value.astype(jnp.float32), axis=0, keepdims=True)
                sums_ref[:, columns] += jnp.broadcast_to(total, (8, width))


def attention_backward(q, k, v, out, grad, lse, start, cos, sin, block=256):
    rows, width = q.shape
    heads = width // HEAD_DIM
    return pl.pallas_call(
        functools.partial(backward_kernel, block),
        grid=(heads,),
        in_specs=[whole((rows, width))] * 5
        + [pl.BlockSpec((1, 8, rows), lambda step: (step, 0, 0)), whole((8, rows)), whole((rows, 128)), whole((rows, 128))],
        out_specs=[whole((rows, 3 * width)), whole((8, 3 * width))],
        out_shape=[
            jax.ShapeDtypeStruct((rows, 3 * width), jnp.bfloat16),
            jax.ShapeDtypeStruct((8, 3 * width), jnp.float32),
        ],
        scratch_shapes=[pltpu.VMEM((rows, width), jnp.float32)] * 3 + [pltpu.VMEM((8, rows), jnp.float32)],
        cost_estimate=pl.CostEstimate(flops=20 * rows * rows * width, bytes_accessed=20 * rows * width, transcendentals=rows * rows * heads // 2),
        name="attention_backward",
    )(q, k, v, out, grad, lse, start, cos, sin)


def small_sums_kernel(
    n_tp, n_dp, norms_ref, heads_ref, out_ref, slots, total, planes, send_one, recv_one, send_two, recv_two
):
    tp, dp = lax.axis_index("tp"), lax.axis_index("dp")
    width = out_ref.shape[1]
    barrier = pltpu.get_barrier_semaphore()
    for hop in range(1, n_tp):
        pl.semaphore_signal(barrier, inc=1, device_id={"tp": lax.rem(tp + hop, n_tp)}, device_id_type=MESH)
    for hop in range(1, n_dp):
        pl.semaphore_signal(barrier, inc=1, device_id={"dp": lax.rem(dp + hop, n_dp)}, device_id_type=MESH)
    pl.semaphore_wait(barrier, n_tp + n_dp - 2)
    copies = []
    for hop in range(1, n_tp):
        peer = lax.rem(tp + hop, n_tp)
        copies.append(
            pltpu.make_async_remote_copy(
                src_ref=norms_ref.at[peer],
                dst_ref=slots.at[hop],
                send_sem=send_one.at[hop],
                recv_sem=recv_one.at[hop],
                device_id={"tp": peer},
                device_id_type=MESH,
            )
        )
    for copy in copies:
        copy.start()
    value = heads_ref[...] + norms_ref[tp]
    for copy in copies:
        copy.wait()
    for hop in range(1, n_tp):
        value = value + slots[hop]
    total[...] = value
    copies = []
    for hop in range(1, n_dp):
        copies.append(
            pltpu.make_async_remote_copy(
                src_ref=total,
                dst_ref=planes.at[dp],
                send_sem=send_two.at[hop],
                recv_sem=recv_two.at[hop],
                device_id={"dp": lax.rem(dp + hop, n_dp)},
                device_id_type=MESH,
            )
        )
    for copy in copies:
        copy.start()
    for copy in copies:
        copy.wait()
    planes[dp] = value
    value = planes[0]
    for plane in range(1, n_dp):
        value = value + planes[plane]
    out_ref[...] = value


def small_sums(norms, heads, n_tp, n_dp):
    width = heads.shape[1]
    return pl.pallas_call(
        functools.partial(small_sums_kernel, n_tp, n_dp),
        in_specs=[pl.BlockSpec(memory_space=pltpu.VMEM)] * 2,
        out_specs=pl.BlockSpec(memory_space=pltpu.VMEM),
        out_shape=jax.ShapeDtypeStruct((8, width), jnp.float32),
        scratch_shapes=[
            pltpu.VMEM((n_tp, 8, width), jnp.float32),
            pltpu.VMEM((8, width), jnp.float32),
            pltpu.VMEM((n_dp, 8, width), jnp.float32),
            pltpu.SemaphoreType.DMA((n_tp,)),
            pltpu.SemaphoreType.DMA((n_tp,)),
            pltpu.SemaphoreType.DMA((n_dp,)),
            pltpu.SemaphoreType.DMA((n_dp,)),
        ],
        compiler_params=pltpu.CompilerParams(collective_id=0, has_side_effects=True),
        name="small_sums",
    )(norms, heads)


def sum_groups(value, n_dp):
    if n_dp != 4:
        return lax.psum(value, "dp").astype(jnp.float32)
    place = lax.axis_index("dp")
    pair = value + lax.ppermute(value, "dp", [(0, 1), (3, 2)])
    full = pair + lax.ppermute(pair, "dp", [(1, 2), (2, 1)])
    outer = lax.ppermute(full, "dp", [(1, 0), (2, 3)])
    return jnp.where((place == 0) | (place == 3), outer, full).astype(jnp.float32)


def local(
    n_dp,
    n_tp,
    layer_input,
    segments,
    norm_gains,
    norm_biases,
    w_qkv,
    qv_bias,
    key_bias,
    w_out,
    w_gate_up,
    w_down,
    out_grad,
):
    segment_ids = segments[0]
    rows = segment_ids.shape[0]
    width = w_qkv.shape[2]
    heads = width // HEAD_DIM
    hidden = w_down.shape[0]
    cos, sin, starts = rotary_tables(segment_ids)
    start_column = jnp.broadcast_to(starts[:, None], (rows, 128))
    start_row = jnp.broadcast_to(starts[None, :], (8, rows))
    qkv_matrix = w_qkv.reshape(D, 3 * width)
    gate_matrix = w_gate_up.reshape(D, 2 * hidden)
    x_float = layer_input.astype(jnp.float32)
    normed_one, hat_one, inverse_one = norm_forward(x_float, norm_gains[0], norm_biases[0])
    rows_one = lax.all_gather(normed_one.astype(jnp.bfloat16), "tp", axis=0, tiled=True)
    portion = lax.all_gather(out_grad, "tp", axis=0, tiled=True)
    key_full = jnp.concatenate([key_bias, jnp.zeros((heads, HEAD_DIM - ROT), jnp.float32)], axis=1)
    bias_all = jnp.concatenate([qv_bias[0], key_full.reshape(width), qv_bias[1]])
    q, k, v = project(rows_one, qkv_matrix, jnp.broadcast_to(bias_all[None], (8, 3 * width)), cos, sin)
    attended, lse = attention_forward(q, k, v, start_column)
    hidden_state = x_float + lax.psum_scatter(
        jnp.dot(attended, w_out, preferred_element_type=jnp.float32).astype(jnp.bfloat16),
        "tp",
        scatter_dimension=0,
        tiled=True,
    ).astype(jnp.float32)
    normed_two, hat_two, inverse_two = norm_forward(hidden_state, norm_gains[1], norm_biases[1])
    rows_two = lax.all_gather(normed_two.astype(jnp.bfloat16), "tp", axis=0, tiled=True)
    gate_up = jnp.dot(rows_two, gate_matrix, preferred_element_type=jnp.float32)
    gate_part = gate_up[:, :hidden]
    up_part = gate_up[:, hidden:]
    sigmoid_gate = jax.nn.sigmoid(gate_part)
    silu_gate = gate_part * sigmoid_gate
    activation = (silu_gate * up_part).astype(jnp.bfloat16)
    grad_down = sum_groups(contract_rows(activation, portion).astype(jnp.bfloat16), n_dp)
    grad_act = contract_cols(portion, w_down)
    grad_gate = grad_act * up_part * sigmoid_gate * (1.0 + gate_part * (1.0 - sigmoid_gate))
    grad_up = grad_act * silu_gate
    grad_pair = jnp.concatenate([grad_gate, grad_up], axis=1).astype(jnp.bfloat16)
    grad_gate_up = jnp.concatenate(
        [
            sum_groups(contract_rows(rows_two[:, part], grad_pair).astype(jnp.bfloat16), n_dp)
            for part in (slice(0, D // 2), slice(D // 2, D))
        ]
    ).reshape(D, 2, hidden)
    grad_normed_two = lax.psum_scatter(
        contract_cols(grad_pair, gate_matrix).astype(jnp.bfloat16), "tp", scatter_dimension=0, tiled=True
    ).astype(jnp.float32)
    output = hidden_state + lax.psum_scatter(
        jnp.dot(activation, w_down, preferred_element_type=jnp.float32).astype(jnp.bfloat16),
        "tp",
        scatter_dimension=0,
        tiled=True,
    ).astype(jnp.float32)
    back_two, gain_two, shift_two = norm_backward(grad_normed_two, hat_two, inverse_two, norm_gains[1])
    grad_hidden = out_grad.astype(jnp.float32) + back_two
    branch = lax.all_gather(grad_hidden.astype(jnp.bfloat16), "tp", axis=0, tiled=True)
    grad_out = sum_groups(contract_rows(attended, branch).astype(jnp.bfloat16), n_dp)
    grad_att = contract_cols(branch, w_out).astype(jnp.bfloat16)
    grad_flat, sums = attention_backward(q, k, v, attended, grad_att, lse, start_row, cos, sin)
    grad_qkv = sum_groups(contract_rows(rows_one, grad_flat).astype(jnp.bfloat16), n_dp).reshape(D, 3, width)
    grad_normed_one = lax.psum_scatter(
        contract_cols(grad_flat, qkv_matrix).astype(jnp.bfloat16), "tp", scatter_dimension=0, tiled=True
    ).astype(jnp.float32)
    back_one, gain_one, shift_one = norm_backward(grad_normed_one, hat_one, inverse_one, norm_gains[0])
    grad_input = grad_hidden + back_one
    norms = jnp.concatenate([jnp.stack([gain_one, gain_two, shift_one, shift_two]), jnp.zeros((4, D), jnp.float32)])
    norms = norms.reshape(8, n_tp, width).transpose(1, 0, 2)
    head_sums = jnp.concatenate(
        [jnp.zeros((4, width), jnp.float32), sums[0].reshape(3, width), jnp.zeros((1, width), jnp.float32)]
    )
    small = small_sums(norms, head_sums, n_tp, n_dp)
    grad_qv = jnp.stack([small[4], small[6]])
    grad_key = small[5].reshape(heads, HEAD_DIM)[:, :ROT]
    return (output, grad_input, grad_qkv, grad_qv, grad_key, grad_out, grad_gate_up, grad_down, small[:2], small[2:4])


def solution(mesh):
    in_specs = (
        P(("dp", "tp"), None),
        P("dp", None),
        P(),
        P(),
        P(None, None, "tp"),
        P(None, "tp"),
        P("tp", None),
        P("tp", None),
        P(None, None, "tp"),
        P("tp", None),
        P(("dp", "tp"), None),
    )
    out_specs = (
        P(("dp", "tp"), None),
        P(("dp", "tp"), None),
        P(None, None, "tp"),
        P(None, "tp"),
        P("tp", None),
        P("tp", None),
        P(None, None, "tp"),
        P("tp", None),
        P(None, "tp"),
        P(None, "tp"),
    )
    body = functools.partial(local, mesh.shape["dp"], mesh.shape["tp"])
    return jax.shard_map(body, mesh=mesh, in_specs=in_specs, out_specs=out_specs, check_vma=False)
```

time: 1490 us -> 1100 us (0.74)
  waiting for transfers between devices: 907 us -> 672 us
  matrix products: 295 us -> 129 us
  Pallas kernels: 0 us -> 103 us
  local copies, waits for them, and re-layouts: 116 us -> 39.1 us
  other arithmetic: 133 us -> 86.3 us
  starting transfers between devices: 0.45 us -> 41.9 us
    psum x1 -> x0, waiting for transfers between devices: 423 us -> none  [local(): lax.psum(grad_qkv.astype(jnp.bfloat16), 'dp').astype(jnp.float32)]
    ppermute x0 -> x15, waiting for transfers between devices: none -> 341 us  [the longest x5 204 us: sum_groups(): pair = value + lax.ppermute(value, 'dp', [(0, 1), (3, 2)])]
    dot_general x38 -> x10, matrix products: 281 us -> 113 us  [the longest x4 51.1 us: contract_cols(): return lax.dot_general(left, right, NT, preferred_element_type=jnp.float32)]
    pallas_call x0 -> x4, Pallas kernels: none -> 103 us  [the longest x1 43.5 us: attention_backward(): pl.pallas_call(functools.partial(backward_kernel, block), grid=(heads,),...]
    unnamed x13 -> x8, waiting for transfers between devices: 69.3 us -> 0.64 us
    convert_element_type x14 -> x3, other arithmetic: 72.3 us -> 7.49 us  [the longest x2 7.41 us: sum_groups(): jnp.where((place == 0) | (place == 3), outer, full).astype(jnp.float32)]
    reduce_scatter x1, waiting for transfers between devices: 61.5 us -> 0.01 us  [local(): lax.psum_scatter(jnp.dot(activation, w_down, preferred_element_type=jnp.f...]
    dynamic_update_slice x8 -> x0, local copies, waits for them, and re-layouts: 46.5 us -> none  [local(): lax.scan(backward_block, (zero_heads, zero_heads), (query_blocks, grad_bl...]
  transfers between devices with their start and end apart: 11 -> 23, of which waited for: 11 -> 14; matrix products, arithmetic and copies ran while one was open for 7% -> 15% of each run, Pallas kernels for 0% -> 1%
where the time goes in v1:
time: 1100 us; the launch traced here: 1090 us
  waiting for transfers between devices  672 us (61%)
  matrix products  129 us (12%)
  Pallas kernels  103 us (9%)
  other arithmetic  86.3 us (8%)
  starting transfers between devices  41.9 us (4%)
  local copies, waits for them, and re-layouts  39.1 us (4%)
  between operations  15.2 us (1%)
    ppermute x5, waiting for transfers between devices, sum_groups(): pair = value + lax.ppermute(value, 'dp', [(0, 1), (3, 2)])  204 us
    ppermute x5, waiting for transfers between devices, sum_groups(): outer = lax.ppermute(full, 'dp', [(1, 0), (2, 3)])  138 us
    reduce_scatter x1, waiting for transfers between devices, local(): lax.psum_scatter(contract_cols(grad_pair, gate_matrix).astype(jnp.bfloat1...  71.6 us
    reduce_scatter x1, waiting for transfers between devices, local(): lax.psum_scatter(jnp.dot(attended, w_out, preferred_element_type=jnp.floa...  71.6 us
    all_gather x1, waiting for transfers between devices, local(): lax.all_gather(grad_hidden.astype(jnp.bfloat16), 'tp', axis=0, tiled=True)  54.4 us
    all_gather x1, waiting for transfers between devices, local(): lax.all_gather(normed_two.astype(jnp.bfloat16), 'tp', axis=0, tiled=True)  53.8 us
    dot_general x4, matrix products, contract_cols(): return lax.dot_general(left, right, NT, preferred_element_type=jnp.float32)  51.1 us
    pallas_call x1, Pallas kernels, attention_backward(): pl.pallas_call(functools.partial(backward_kernel, block), grid=(heads,),...  43.5 us
  transfers between devices with their start and end apart: 23, of which 14 were waited for; matrix products, arithmetic and copies ran while one was open for 15% of the time, Pallas kernels for 1%

profile of v1, /device:TPU:0, one launch (start us, length us, event | category | flops | bytes accessed | tf_op | source)
XLA Modules:
  0.0 1086.8 jit_solution(3061623785252187119)
XLA Ops:
  14.4 4.6 copy.24
  19.1 4.6 copy.25.w_ref
  24.0 5.5 fusion.35
  29.5 41.3 %all-gather.5.cloned.1.call-done.x_ref = bf16[2048,2048]{1,0:T(8,128)(2,1)} async-done(((bf16[256,2048]{1,0:T(8,128)(2,1)}), bf16[2048,2048]{1,0:T(8,128)(2,1)}) %all-gather.5.cloned.1.call-update) | async-done | bytes 8388624 | tf_op jit(solution)/shard_map/all_gather | solution.py:337
  71.4 11.7 %project.1 = (bf16[2048,256]{1,0:T(8,128)(2,1)}, bf16[2048,256]{1,0:T(8,128)(2,1)}, bf16[2048,256]{1,0:T(8,128)(2,1)}) custom-call(bf16[2048,2048]{1,0:T(8,128)(2,1)} %all-gather.5.cloned.1.call-done.x_ref, bf16[2048,768]{1,0:T(8,128)(2,1)} %copy.25.w_ref, f32[8,768]{1,0:T(8,128)} %broadcast_in_dim.28.bias_ref, f32[2048,128]{1,0:T(8,128)} %get-tuple-element.64.cos_ref, ...), custom_call_target="tpu_custom_call" | custom-call | flops 6442450944 | bytes 14680064 | tf_op jit(solution)/shard_map/project/pallas_call | solution.py:88
  84.4 37.8 %attention_forward.1 = (bf16[2048,256]{1,0:T(8,128)(2,1)}, f32[4,8,2048]{2,1,0:T(8,128)}) custom-call(bf16[2048,256]{1,0:T(8,128)(2,1)} %get-tuple-element.17.q_ref, bf16[2048,256]{1,0:T(8,128)(2,1)} %get-tuple-element.18.k_ref, bf16[2048,256]{1,0:T(8,128)(2,1)} %get-tuple-element.19.v_ref, s32[2048,128]{1,0:T(8,128)} %broadcast_in_dim.33.start_ref), custom_call_target="tpu_custom_call" | custom-call | flops 8589934592 | bytes 6291456 | tf_op jit(solution)/shard_map/attention_forward/pallas_call | solution.py:132
  122.2 7.3 convolution_convert_fusion.3
  129.5 71.6 %reduce-scatter.5.cloned.1.call-done = bf16[256,2048]{1,0:T(8,128)(2,1)} async-done(((bf16[2048,2048]{1,0:T(8,128)(2,1)}), bf16[256,2048]{1,0:T(8,128)(2,1)}) %reduce-scatter.5.cloned.1.call-update) | async-done | bytes 1048592 | tf_op jit(solution)/shard_map/reduce_scatter | solution.py:343
  201.1 2.0 fusion.34
  203.2 2.0 multiply_reduce_fusion
  207.5 53.8 %all-gather.7.cloned.1.call-done = bf16[2048,2048]{1,0:T(8,128)(2,1)} async-done(((bf16[256,2048]{1,0:T(8,128)(2,1)}), bf16[2048,2048]{1,0:T(8,128)(2,1)}) %all-gather.7.cloned.1.call-update) | async-done | bytes 8388624 | tf_op jit(solution)/shard_map/all_gather | solution.py:350
  261.2 18.8 %fusion.48 = f32[2048,1408]{0,1:T(8,128)} fusion(bf16[2048,2048]{1,0:T(8,128)(2,1)} %all-gather.7.cloned.1.call-done, bf16[2048,1408]{0,1:T(8,128)(2,1)} %bitcast.69), kind=kOutput, calls=%fused_computation.103 | convolution fusion | flops 11811160064 | bytes 25690112 | tf_op jit(solution)/shard_map/dot_general | solution.py:351
  280.1 37.2 %all-gather.9.cloned.1.call-done = bf16[2048,2048]{1,0:T(8,128)(2,1)} async-done(((bf16[256,2048]{1,0:T(8,128)(2,1)}), bf16[2048,2048]{1,0:T(8,128)(2,1)}) %all-gather.9.cloned.1.call-update) | async-done | bytes 8388624 | tf_op jit(solution)/shard_map/all_gather | solution.py:338
  317.3 14.5 %multiply_convert_fusion.1 = (bf16[2048,704]{0,1:T(8,128)(2,1)S(1)}, bf16[2048,704]{0,1:T(8,128)(2,1)S(1)}, bf16[2048,704]{0,1:T(8,128)(2,1)}) fusion(f32[2048,1408]{0,1:T(8,128)} %fusion.48, bf16[2048,2048]{1,0:T(8,128)(2,1)} %all-gather.9.cloned.1.call-done, bf16[704,2048]{1,0:T(8,128)(2,1)S(1)} %copy-done), kind=kOutput, calls=%fused_computation.7 | convolution fusion | flops 5927206912 | bytes 31457280 | tf_op jit(solution)/shard_map/dot_general | solution.py:45
  334.4 17.9 %convolution_convert_fusion.1 = bf16[2048,2048]{1,0:T(8,128)(2,1)} fusion(bf16[2048,1408]{0,1:T(8,128)(2,1)} %bitcast.70, bf16[2048,704]{0,1:T(8,128)(2,1)S(1)} %get-tuple-element.55, bf16[2048,704]{0,1:T(8,128)(2,1)S(1)} %get-tuple-element.54), kind=kOutput, calls=%fused_computation.1 | convolution fusion | flops 11826888704 | bytes 19922944 | tf_op jit(solution)/shard_map/dot_general | solution.py:45
  352.3 71.6 %reduce-scatter.9.cloned.1.call-done = bf16[256,2048]{1,0:T(8,128)(2,1)} async-done(((bf16[2048,2048]{1,0:T(8,128)(2,1)}), bf16[256,2048]{1,0:T(8,128)(2,1)}) %reduce-scatter.9.cloned.1.call-update) | async-done | bytes 1048592 | tf_op jit(solution)/shard_map/reduce_scatter | solution.py:368
  423.9 3.7 fusion.32
  428.7 3.4 fusion.43
  432.2 54.4 %all-gather.11.cloned.1.call-done = bf16[2048,2048]{1,0:T(8,128)(2,1)} async-done(((bf16[256,2048]{1,0:T(8,128)(2,1)}), bf16[2048,2048]{1,0:T(8,128)(2,1)}) %all-gather.11.cloned.1.call-update) | async-done | bytes 8388624 | tf_op jit(solution)/shard_map/all_gather | solution.py:379
  486.5 7.0 convolution_convert_fusion.7.g_ref
  494.1 43.5 %attention_backward.1 = (bf16[2048,768]{1,0:T(8,128)(2,1)}, f32[8,768]{1,0:T(8,128)}) custom-call(bf16[2048,256]{1,0:T(8,128)(2,1)} %get-tuple-element.17.q_ref, bf16[2048,256]{1,0:T(8,128)(2,1)} %get-tuple-element.18.k_ref, bf16[2048,256]{1,0:T(8,128)(2,1)} %get-tuple-element.19.v_ref, bf16[2048,256]{1,0:T(8,128)(2,1)} %get-tuple-element.20.o_ref, ...), custom_call_target="tpu_custom_call" | custom-call | flops 21474836480 | bytes 10485760 | tf_op jit(solution)/shard_map/attention_backward/pallas_call | solution.py:208
  537.6 11.7 %convolution_convert_fusion = bf16[2048,2048]{1,0:T(8,128)(2,1)} fusion(bf16[2048,768]{1,0:T(8,128)(2,1)} %get-tuple-element.22, bf16[2048,768]{0,1:T(8,128)(2,1)} %bitcast.47), kind=kOutput, calls=%fused_computation | convolution fusion | flops 6446645248 | bytes 14680064 | tf_op jit(solution)/shard_map/dot_general | solution.py:45
  549.4 11.8 %fusion.8 = bf16[1024,1408]{1,0:T(8,128)(2,1)} fusion(bf16[2048,2048]{1,0:T(8,128)(2,1)} %all-gather.7.cloned.1.call-done, bf16[2048,704]{0,1:T(8,128)(2,1)} %copy-done.34, bf16[2048,704]{0,1:T(8,128)(2,1)} %copy-done.32), kind=kOutput, calls=%fused_computation.16 | convolution fusion | flops 5918556160 | bytes 12845056 | tf_op jit(solution)/shard_map/dot_general | solution.py:41
  561.2 5.4 collective-permute-start.9
  566.6 9.8 fusion.5
  576.4 2.9 collective-permute-start.6
  579.3 7.7 convolution_convert_fusion.5
  587.0 9.0 convolution_convert_fusion.2
  596.0 2.9 collective-permute-start.12
  598.9 29.2 %collective-permute-done.9 = bf16[1024,1408]{1,0:T(8,128)(2,1)} collective-permute-done((bf16[1024,1408]{1,0:T(8,128)(2,1)}, bf16[1024,1408]{1,0:T(8,128)(2,1)}, u32[]{:S(2)}, u32[]{:S(2)}) %collective-permute-start.9) | collective-permute-done | bytes 2883616 | tf_op jit(solution)/shard_map/ppermute | solution.py:304
  628.1 4.1 add.140
  633.1 10.2 convolution_convert_fusion.4
  643.3 7.3 collective-permute-start
  650.6 39.4 %collective-permute-done.6 = bf16[1024,1408]{1,0:T(8,128)(2,1)} collective-permute-done((bf16[1024,1408]{1,0:T(8,128)(2,1)}, bf16[1024,1408]{1,0:T(8,128)(2,1)}, u32[]{:S(2)}, u32[]{:S(2)}) %collective-permute-start.6) | collective-permute-done | bytes 2883616 | tf_op jit(solution)/shard_map/ppermute | solution.py:304
  689.9 3.5 add.138
  694.5 57.3 %collective-permute-done.12 = bf16[704,2048]{1,0:T(8,128)(2,1)} collective-permute-done((bf16[704,2048]{1,0:T(8,128)(2,1)}, bf16[704,2048]{1,0:T(8,128)(2,1)}, u32[]{:S(2)}, u32[]{:S(2)}) %collective-permute-start.12) | collective-permute-done | bytes 2883616 | tf_op jit(solution)/shard_map/ppermute | solution.py:304
  751.7 3.0 add.142
  755.6 2.3 add.141
  759.2 59.1 %collective-permute-done = bf16[2048,768]{0,1:T(8,128)(2,1)S(1)} collective-permute-done((bf16[2048,768]{0,1:T(8,128)(2,1)S(1)}, bf16[2048,768]{0,1:T(8,128)(2,1)S(1)}, u32[]{:S(2)}, u32[]{:S(2)}) %collective-permute-start) | collective-permute-done | bytes 3145760 | tf_op jit(solution)/shard_map/ppermute | solution.py:304
  818.3 3.1 add.134
  821.4 2.3 collective-permute-start.1
  823.7 2.3 add.139
  827.6 2.8 add.143
  831.7 3.3 convolution_convert_fusion.6
  835.1 9.6 collective-permute-start.3
  844.7 2.1 broadcast_select_fusion.1
  846.9 18.8 %collective-permute-done.3 = bf16[256,2048]{1,0:T(8,128)(2,1)} collective-permute-done((bf16[256,2048]{1,0:T(8,128)(2,1)}, bf16[256,2048]{1,0:T(8,128)(2,1)}, u32[]{:S(2)}, u32[]{:S(2)}) %collective-permute-start.3) | collective-permute-done | bytes 1048608 | tf_op jit(solution)/shard_map/ppermute | solution.py:304
  865.7 2.9 add.136
  868.6 1.7 collective-permute-start.4
  870.2 6.1 add.135
  877.6 17.1 %collective-permute-done.8 = bf16[1024,1408]{1,0:T(8,128)(2,1)} collective-permute-done((bf16[1024,1408]{1,0:T(8,128)(2,1)}, bf16[1024,1408]{1,0:T(8,128)(2,1)}, u32[]{:S(2)}, u32[]{:S(2)}) %collective-permute-start.8) | collective-permute-done | bytes 2883616 | tf_op jit(solution)/shard_map/ppermute | solution.py:306
  894.8 2.1 broadcast_select_fusion.2
  896.9 5.0 maximum_convert_fusion
  901.9 11.9 %copy.26 = f32[2048,1408]{0,1:T(8,128)} copy(f32[2048,1408]{1,0:T(8,128)} %maximum_convert_fusion) | data formatting | bytes 23068672 | tf_op jit(solution)/shard_map/reshape | solution.py:367
  913.9 2.9 add.137
  918.3 38.3 %collective-permute-done.14 = bf16[704,2048]{1,0:T(8,128)(2,1)} collective-permute-done((bf16[704,2048]{1,0:T(8,128)(2,1)}, bf16[704,2048]{1,0:T(8,128)(2,1)}, u32[]{:S(2)}, u32[]{:S(2)}) %collective-permute-start.14) | collective-permute-done | bytes 2883616 | tf_op jit(solution)/shard_map/ppermute | solution.py:306
  956.6 4.7 select_convert_fusion
  962.7 82.1 %collective-permute-done.5 = bf16[256,2048]{1,0:T(8,128)(2,1)} collective-permute-done((bf16[256,2048]{1,0:T(8,128)(2,1)}, bf16[256,2048]{1,0:T(8,128)(2,1)}, u32[]{:S(2)}, u32[]{:S(2)}) %collective-permute-start.5) | collective-permute-done | bytes 1048608 | tf_op jit(solution)/shard_map/ppermute | solution.py:306
  1044.9 2.7 select_convert_fusion.1
  1047.6 3.9 broadcast_select_fusion
  1051.5 5.4 copy.27
  1056.9 2.6 fusion.33
  1060.2 10.4 small_sums.1
  1074.1 5.4 fusion.25
  (156 shorter events, 31.3 us)
Async XLA Ops:
  7.2 310.1 %copy-start = (bf16[704,2048]{1,0:T(8,128)(2,1)S(1)}, bf16[704,2048]{1,0:T(8,128)(2,1)}, u32[]{:S(2)}) copy-start(bf16[704,2048]{1,0:T(8,128)(2,1)} %param.20) | copy-start | bytes 8650756
  7.2 6.5 copy-start.28
  7.2 6.6 copy-start.17
  7.2 63.6 %all-gather.5.cloned.1.call-start = ((), (), s32[]{:S(2)}) async-start(), calls=%async_computation.4 | async-start | bytes 9437184 | tf_op jit(solution)/shard_map/all_gather | solution.py:337
  7.3 5.0 copy-start.1
  8.9 5.4 copy-start.18
  10.5 3.8 copy-start.22
  11.4 0.8 copy-start.11
  11.4 416.3 %copy-start.9 = (f32[1,2048]{1,0:T(1,128)}, f32[1,2048]{1,0:T(1,128)S(1)}, u32[]{:S(2)}) copy-start(f32[1,2048]{1,0:T(1,128)S(1)} %get-tuple-element.60) | copy-start | bytes 24580
  13.7 187.5 %reduce-scatter.5.cloned.1.call-start = ((), (), s32[]{:S(2)}) async-start(), calls=%async_computation.5 | async-start | bytes 9437184 | tf_op jit(solution)/shard_map/reduce_scatter | solution.py:343
  19.1 4.7 copy-start.29
  129.5 131.7 %all-gather.7.cloned.1.call-start = ((), (), s32[]{:S(2)}) async-start(), calls=%async_computation.6 | async-start | bytes 9437184 | tf_op jit(solution)/shard_map/all_gather | solution.py:350
  201.1 4.1 copy-start.2
  201.1 4.1 copy-start.4
  203.2 224.5 %copy-start.13 = (f32[256]{0:T(256)}, f32[256]{0:T(256)S(1)}, u32[]{:S(2)}) copy-start(f32[256]{0:T(256)S(1)} %broadcast_multiply_fusion.4) | copy-start | bytes 3076
  205.3 222.4 %copy-start.20 = (f32[256]{0:T(256)}, f32[256]{0:T(256)S(1)}, u32[]{:S(2)}) copy-start(f32[256]{0:T(256)S(1)} %add_rsqrt_fusion) | copy-start | bytes 3076
  206.8 110.4 %all-gather.9.cloned.1.call-start = ((), (), s32[]{:S(2)}) async-start(), calls=%async_computation.8 | async-start | bytes 9437184 | tf_op jit(solution)/shard_map/all_gather | solution.py:338
  207.4 216.5 %reduce-scatter.9.cloned.1.call-start = ((), (), s32[]{:S(2)}) async-start(), calls=%async_computation.9 | async-start | bytes 9437184 | tf_op jit(solution)/shard_map/reduce_scatter | solution.py:368
  331.8 1.6 copy-start.32
  331.8 2.6 copy-start.34
  352.3 134.2 %all-gather.11.cloned.1.call-start = ((), (), s32[]{:S(2)}) async-start(), calls=%async_computation.10 | async-start | bytes 9437184 | tf_op jit(solution)/shard_map/all_gather | solution.py:379
  423.9 4.8 copy-start.3
  423.9 4.8 copy-start.5
  423.9 4.8 copy-start.6
  427.7 0.5 copy-start.24
  428.2 0.5 copy-start.26
  432.1 624.8 %reduce-scatter.11.cloned.1.call-start = ((), (), s32[]{:S(2)}) async-start(), calls=%async_computation.11 | async-start | bytes 9437184 | tf_op jit(solution)/shard_map/reduce_scatter | solution.py:384
  549.3 524.8 %reduce-scatter.7.cloned.1.call-start = ((), (), s32[]{:S(2)}) async-start(), calls=%async_computation.7 | async-start | bytes 9437184 | tf_op jit(solution)/shard_map/reduce_scatter | solution.py:371
  549.4 17.2 %copy-start.33 = (bf16[2048,704]{0,1:T(8,128)(2,1)S(1)}, bf16[2048,704]{0,1:T(8,128)(2,1)}, u32[]{:S(2)}) copy-start(bf16[2048,704]{0,1:T(8,128)(2,1)} %copy-done.32) | copy-start | bytes 8650756
  549.4 17.2 %copy-start.35 = (bf16[2048,704]{0,1:T(8,128)(2,1)S(1)}, bf16[2048,704]{0,1:T(8,128)(2,1)}, u32[]{:S(2)}) copy-start(bf16[2048,704]{0,1:T(8,128)(2,1)} %copy-done.34) | copy-start | bytes 8650756
  549.4 29.9 %slice-start.2 = ((s8[8388608]{0:T(1024)(128)(4,1)}), s8[4194304]{0:T(1024)(128)(4,1)S(1)}, s32[]{:S(2)}) async-start(s8[8388608]{0:T(1024)(128)(4,1)} %bitcast.67), calls=%async_computation.14 | async-start | bytes 8388608
  561.2 18.1 %slice-start.3 = ((s8[8388608]{0:T(1024)(128)(4,1)}), s8[4194304]{0:T(1024)(128)(4,1)S(1)}, s32[]{:S(2)}) async-start(s8[8388608]{0:T(1024)(128)(4,1)} %bitcast.67), calls=%async_computation.15 | async-start | bytes 8388608
  561.2 18.1 %copy-start.30 = (bf16[2048,704]{0,1:T(8,128)(2,1)S(1)}, bf16[2048,704]{0,1:T(8,128)(2,1)}, u32[]{:S(2)}) copy-start(bf16[2048,704]{0,1:T(8,128)(2,1)} %get-tuple-element.56) | copy-start | bytes 8650756
  561.2 67.0 %collective-permute-start.9 = (bf16[1024,1408]{1,0:T(8,128)(2,1)}, bf16[1024,1408]{1,0:T(8,128)(2,1)}, u32[]{:S(2)}, u32[]{:S(2)}) collective-permute-start(bf16[1024,1408]{1,0:T(8,128)(2,1)} %fusion.8), channel_id=1, source_target_pairs={{0,8},{24,16},{1,9},{25,17},{2,10},{26,18},{3,11},{27,19},{4,12},{... | collective-permute-start | bytes 8650760 | tf_op jit(solution)/shard_map/ppermute | solution.py:304
  576.4 113.5 %collective-permute-start.6 = (bf16[1024,1408]{1,0:T(8,128)(2,1)}, bf16[1024,1408]{1,0:T(8,128)(2,1)}, u32[]{:S(2)}, u32[]{:S(2)}) collective-permute-start(bf16[1024,1408]{1,0:T(8,128)(2,1)} %fusion.5), channel_id=1, source_target_pairs={{0,8},{24,16},{1,9},{25,17},{2,10},{26,18},{3,11},{27,19},{4,12},{... | collective-permute-start | bytes 8650760 | tf_op jit(solution)/shard_map/ppermute | solution.py:304
  596.0 155.7 %collective-permute-start.12 = (bf16[704,2048]{1,0:T(8,128)(2,1)}, bf16[704,2048]{1,0:T(8,128)(2,1)}, u32[]{:S(2)}, u32[]{:S(2)}) collective-permute-start(bf16[704,2048]{1,0:T(8,128)(2,1)} %convolution_convert_fusion.5), channel_id=1, source_target_pairs={{0,8},{24,16},{1,9},{25,17},{2,10},{26,18},{3,11},{27,19},{4,12},{... | collective-permute-start | bytes 8650760 | tf_op jit(solution)/shard_map/ppermute | solution.py:304
  598.9 34.2 %copy-start.31 = (bf16[2048,768]{1,0:T(8,128)(2,1)S(1)}, bf16[2048,768]{1,0:T(8,128)(2,1)}, u32[]{:S(2)}) copy-start(bf16[2048,768]{1,0:T(8,128)(2,1)} %get-tuple-element.22) | copy-start | bytes 9437188
  632.2 123.4 %collective-permute-start.10 = (bf16[1024,1408]{1,0:T(8,128)(2,1)S(1)}, bf16[1024,1408]{1,0:T(8,128)(2,1)S(1)}, u32[]{:S(2)}, u32[]{:S(2)}) collective-permute-start(bf16[1024,1408]{1,0:T(8,128)(2,1)S(1)} %add.140), channel_id=1, source_target_pairs={{8,16},{16,8},{9,17},{17,9},{10,18},{18,10},{11,19},{19,11},{12,20... | collective-permute-start | bytes 8650760 | tf_op jit(solution)/shard_map/ppermute | solution.py:305
  643.3 108.5 %copy-start.8 = (bf16[704,2048]{1,0:T(8,128)(2,1)S(1)}, bf16[704,2048]{1,0:T(8,128)(2,1)}, u32[]{:S(2)}) copy-start(bf16[704,2048]{1,0:T(8,128)(2,1)} %convolution_convert_fusion.5) | copy-start | bytes 8650756
  643.3 175.1 %collective-permute-start = (bf16[2048,768]{0,1:T(8,128)(2,1)S(1)}, bf16[2048,768]{0,1:T(8,128)(2,1)S(1)}, u32[]{:S(2)}, u32[]{:S(2)}) collective-permute-start(bf16[2048,768]{0,1:T(8,128)(2,1)S(1)} %convolution_convert_fusion.4), channel_id=1, source_target_pairs={{0,8},{24,16},{1,9},{25,17},{2,10},{26,18},{3,11},{27,19},{4,12},{... | collective-permute-start | bytes 9437192 | tf_op jit(solution)/shard_map/ppermute | solution.py:304
  693.4 130.3 %collective-permute-start.7 = (bf16[1024,1408]{1,0:T(8,128)(2,1)S(1)}, bf16[1024,1408]{1,0:T(8,128)(2,1)S(1)}, u32[]{:S(2)}, u32[]{:S(2)}) collective-permute-start(bf16[1024,1408]{1,0:T(8,128)(2,1)S(1)} %add.138), channel_id=1, source_target_pairs={{8,16},{16,8},{9,17},{17,9},{10,18},{18,10},{11,19},{19,11},{12,20... | collective-permute-start | bytes 8650760 | tf_op jit(solution)/shard_map/ppermute | solution.py:305
  754.8 72.8 %collective-permute-start.13 = (bf16[704,2048]{1,0:T(8,128)(2,1)S(1)}, bf16[704,2048]{1,0:T(8,128)(2,1)S(1)}, u32[]{:S(2)}, u32[]{:S(2)}) collective-permute-start(bf16[704,2048]{1,0:T(8,128)(2,1)S(1)} %add.142), channel_id=1, source_target_pairs={{8,16},{16,8},{9,17},{17,9},{10,18},{18,10},{11,19},{19,11},{12,20... | collective-permute-start | bytes 8650760 | tf_op jit(solution)/shard_map/ppermute | solution.py:305
  757.9 86.8 %collective-permute-start.11 = (bf16[1024,1408]{1,0:T(8,128)(2,1)}, bf16[1024,1408]{1,0:T(8,128)(2,1)}, u32[]{:S(2)}, u32[]{:S(2)}) collective-permute-start(bf16[1024,1408]{1,0:T(8,128)(2,1)} %add.141), channel_id=1, source_target_pairs={{8,0},{16,24},{9,1},{17,25},{10,2},{18,26},{11,3},{19,27},{12,4},{... | collective-permute-start | bytes 8650760 | tf_op jit(solution)/shard_map/ppermute | solution.py:306
  821.4 48.8 %collective-permute-start.1 = (bf16[2048,768]{0,1:T(8,128)(2,1)}, bf16[2048,768]{0,1:T(8,128)(2,1)}, u32[]{:S(2)}, u32[]{:S(2)}) collective-permute-start(bf16[2048,768]{0,1:T(8,128)(2,1)} %add.134), channel_id=1, source_target_pairs={{8,16},{16,8},{9,17},{17,9},{10,18},{18,10},{11,19},{19,11},{12,20... | collective-permute-start | bytes 9437192 | tf_op jit(solution)/shard_map/ppermute | solution.py:305
  823.7 8.0 slice-start
  826.0 5.7 slice-start.1
  826.0 5.7 copy-start.7
  826.0 68.8 %collective-permute-start.8 = (bf16[1024,1408]{1,0:T(8,128)(2,1)}, bf16[1024,1408]{1,0:T(8,128)(2,1)}, u32[]{:S(2)}, u32[]{:S(2)}) collective-permute-start(bf16[1024,1408]{1,0:T(8,128)(2,1)} %add.139), channel_id=1, source_target_pairs={{8,0},{16,24},{9,1},{17,25},{10,2},{18,26},{11,3},{19,27},{12,4},{... | collective-permute-start | bytes 8650760 | tf_op jit(solution)/shard_map/ppermute | solution.py:306
  830.4 126.2 %collective-permute-start.14 = (bf16[704,2048]{1,0:T(8,128)(2,1)}, bf16[704,2048]{1,0:T(8,128)(2,1)}, u32[]{:S(2)}, u32[]{:S(2)}) collective-permute-start(bf16[704,2048]{1,0:T(8,128)(2,1)} %add.143), channel_id=1, source_target_pairs={{8,0},{16,24},{9,1},{17,25},{10,2},{18,26},{11,3},{19,27},{12,4},{... | collective-permute-start | bytes 8650760 | tf_op jit(solution)/shard_map/ppermute | solution.py:306
  835.1 30.6 %collective-permute-start.3 = (bf16[256,2048]{1,0:T(8,128)(2,1)}, bf16[256,2048]{1,0:T(8,128)(2,1)}, u32[]{:S(2)}, u32[]{:S(2)}) collective-permute-start(bf16[256,2048]{1,0:T(8,128)(2,1)} %convolution_convert_fusion.6), channel_id=1, source_target_pairs={{0,8},{24,16},{1,9},{25,17},{2,10},{26,18},{3,11},{27,19},{4,12},{... | collective-permute-start | bytes 3145736 | tf_op jit(solution)/shard_map/ppermute | solution.py:304
  868.6 45.3 %collective-permute-start.4 = (bf16[256,2048]{1,0:T(8,128)(2,1)}, bf16[256,2048]{1,0:T(8,128)(2,1)}, u32[]{:S(2)}, u32[]{:S(2)}) collective-permute-start(bf16[256,2048]{1,0:T(8,128)(2,1)} %add.136), channel_id=1, source_target_pairs={{8,16},{16,8},{9,17},{17,9},{10,18},{18,10},{11,19},{19,11},{12,20... | collective-permute-start | bytes 3145736 | tf_op jit(solution)/shard_map/ppermute | solution.py:305
  876.3 171.2 %collective-permute-start.2 = (bf16[2048,768]{0,1:T(8,128)(2,1)}, bf16[2048,768]{0,1:T(8,128)(2,1)}, u32[]{:S(2)}, u32[]{:S(2)}) collective-permute-start(bf16[2048,768]{0,1:T(8,128)(2,1)} %add.135), channel_id=1, source_target_pairs={{8,0},{16,24},{9,1},{17,25},{10,2},{18,26},{11,3},{19,27},{12,4},{... | collective-permute-start | bytes 9437192 | tf_op jit(solution)/shard_map/ppermute | solution.py:306
  916.8 128.1 %collective-permute-start.5 = (bf16[256,2048]{1,0:T(8,128)(2,1)}, bf16[256,2048]{1,0:T(8,128)(2,1)}, u32[]{:S(2)}, u32[]{:S(2)}) collective-permute-start(bf16[256,2048]{1,0:T(8,128)(2,1)} %add.137), channel_id=1, source_target_pairs={{8,0},{16,24},{9,1},{17,25},{10,2},{18,26},{11,3},{19,27},{12,4},{... | collective-permute-start | bytes 3145736 | tf_op jit(solution)/shard_map/ppermute | solution.py:306
  1051.4 5.5 copy-start.12
  1051.4 5.5 copy-start.19
  1051.4 5.5 copy-start.23
  1051.4 8.1 copy-start.15
  1051.4 8.1 copy-start.16
  1051.4 22.6 %copy-start.10 = (f32[1,2048]{1,0:T(1,128)S(1)}, f32[1,2048]{1,0:T(1,128)}, u32[]{:S(2)}) copy-start(f32[1,2048]{1,0:T(1,128)} %copy-done.9) | copy-start | bytes 24580
  1051.5 22.6 %copy-start.14 = (f32[256]{0:T(256)S(1)}, f32[256]{0:T(256)}, u32[]{:S(2)}) copy-start(f32[256]{0:T(256)} %copy-done.13) | copy-start | bytes 3076
  1051.5 22.6 %copy-start.21 = (f32[256]{0:T(256)S(1)}, f32[256]{0:T(256)}, u32[]{:S(2)}) copy-start(f32[256]{0:T(256)} %copy-done.20) | copy-start | bytes 3076
  1051.5 22.6 %copy-start.25 = (f32[256]{0:T(256)S(1)}, f32[256]{0:T(256)}, u32[]{:S(2)}) copy-start(f32[256]{0:T(256)} %copy-done.24) | copy-start | bytes 3076
  1051.5 22.6 %copy-start.27 = (f32[256]{0:T(256)S(1)}, f32[256]{0:T(256)}, u32[]{:S(2)}) copy-start(f32[256]{0:T(256)} %copy-done.26) | copy-start | bytes 3076
Sparse Core Ops, SparseCore 0:
  13.8 56.9 all-gather.4
  129.6 71.4 reduce-scatter.4
  207.0 54.2 all-gather.6
  263.0 54.2 all-gather.8
  352.4 71.4 reduce-scatter.8
  432.2 54.2 all-gather.10
  549.5 71.5 reduce-scatter.10
  624.5 71.4 reduce-scatter.6
